TPU v7x, 512 devices: a whole 4x8x8 slice. The times are simulated.
512 devices in a mesh: blk: 64 (over y, x, z_lo), ga: 8 (over z_hi, core).
Axes of the slice: x: 4, y: 8, z: 8 (z_hi: 4, z_lo: 2; z = z_hi * 2 + z_lo), core: 2. Of those that a mesh axis runs over, the one named last changes fastest.
Arguments:
- pair_elements: bfloat16 [4096, 65536], P('ga', 'blk'), may hold values from -6 to 6
- screening: bfloat16 [4096, 4096], P('ga', 'blk'), may hold values from -0.09375 to 0.09375
- energies: float32 [1024], replicated, may hold values from 0.5 to 3
- frequencies: float32 [8], replicated, may hold values from 0.3 to 3
- qp_index: int32 [32], replicated, may hold values from 0 to 1023
- occupied: int32 [1024], replicated, may hold values 0 or 1
Outputs:
- self_energy: float32 [2, 8, 32, 32], replicated
All inputs are finite; a program needn't handle non-finite values.
Results may differ from a plain program's by a relative error of at most 0.0003.
Values may be sent and summed in bfloat16 or wider, within the bound.
A program may use at most 64 MiB of HBM per device.

v0:
```python
import jax
import jax.numpy as jnp
from jax import lax
from jax.sharding import Mesh
from jax.sharding import PartitionSpec as P

STATES = 32
NG = 4096
BLK = ("blk_0", "blk_1", "blk_2")
BLK_GA = ("blk_0", "blk_1", "blk_2", "ga")


def laid_out(pieces, dim):
    dims = list(pieces.shape[1:])
    dims[dim] *= pieces.shape[0]
    return jnp.moveaxis(pieces, 0, dim).reshape(dims)


def all_blocks(shard, axes, order):
    pieces = shard[None]
    for k in order:
        pieces = lax.all_gather(pieces, axes[k], axis=0, tiled=True)
    block = [lax.axis_size(axes[k]) for k in reversed(order)]
    pieces = pieces.reshape(*block, *shard.shape)
    turned = sorted(range(len(order)), key=lambda place: order[len(order) - 1 - place])
    return pieces.transpose(*turned, *range(len(order), pieces.ndim)).reshape(-1, *shard.shape)


def gathered_by_axis(shard, axes, order, dim):
    return laid_out(all_blocks(shard, axes, order), dim)


def band_weights(energies, frequencies, qp_index, occupied, offset, band_count):
    level_count = energies.shape[0]
    position = jnp.arange(level_count, dtype=jnp.int32)
    signed = jnp.where(occupied == 1, -energies, energies)
    onehot = (qp_index[:, None] == position[None, :]).astype(jnp.float32)
    state_level = jnp.sum(onehot * signed[None, :], axis=1)
    band_level = lax.dynamic_slice_in_dim(signed, offset, band_count, 0)
    detuning = state_level[:, None] - band_level[None, :]
    imag_freq = frequencies[:, None, None]
    modulus = detuning[None] ** 2 + imag_freq**2
    return (detuning[None] / modulus, -imag_freq / modulus)


def window_sigma(elements, screened, weight_real, weight_imag, band_count):
    row_count = elements.shape[0]
    local_elems = elements.astype(jnp.float32).reshape(row_count, band_count, 2, STATES)
    image_cols = screened.reshape(row_count, band_count, 2, STATES)
    intersection = jnp.einsum(
        "gnpi,gnqj->npiqj", local_elems, image_cols, precision=lax.Precision.HIGHEST
    )
    intersection_real = intersection[:, 0, :, 0, :] + intersection[:, 1, :, 1, :]
    intersection_imag = intersection[:, 0, :, 1, :] - intersection[:, 1, :, 0, :]
    sigma_real = jnp.einsum(
        "kin,nij->kij", weight_real, intersection_real, precision=lax.Precision.HIGHEST
    ) - jnp.einsum("kin,nij->kij", weight_imag, intersection_imag, precision=lax.Precision.HIGHEST)
    sigma_imag = jnp.einsum(
        "kin,nij->kij", weight_real, intersection_imag, precision=lax.Precision.HIGHEST
    ) + jnp.einsum("kin,nij->kij", weight_imag, intersection_real, precision=lax.Precision.HIGHEST)
    return jnp.stack([sigma_real, sigma_imag]) / NG


def shards(pair_elements, screening, energies, frequencies, qp_index, occupied):
    col_count = pair_elements.shape[1]
    band_count = col_count // (2 * STATES)
    gathered = lax.all_gather(pair_elements, "ga", axis=0, tiled=True)
    screened = jnp.dot(
        gathered_by_axis(screening, BLK, (2, 0, 1), 1), gathered, preferred_element_type=jnp.float32
    )
    band_start = lax.axis_index(BLK) * band_count
    weight_real, weight_imag = band_weights(
        energies, frequencies, qp_index, occupied, band_start, band_count
    )
    partial_value = window_sigma(pair_elements, screened, weight_real, weight_imag, band_count)
    return lax.psum(partial_value, BLK_GA)


def solution(mesh):
    torus = Mesh(mesh.devices.reshape(8, 4, 2, mesh.shape["ga"]), ("blk_0", "blk_1", "blk_2", "ga"))
    in_specs = (P("ga", BLK), P("ga", BLK), P(), P(), P(), P())
    out_specs = P()
    return jax.shard_map(
        shards, mesh=torus, in_specs=in_specs, out_specs=out_specs, check_vma=False
    )
```

profile of v0, /device:TPU:23, one launch (start us, length us, event | category | flops | bytes accessed | tf_op | source)
XLA Modules:
  0.0 498.5 jit_solution(6160109027785036022)
XLA Ops:
  6.6 4.7 all-gather
  11.3 0.7 copy.75
  12.0 0.0 all-gather.7.cloned.1.call-start
  12.0 40.0 %all-gather.5.cloned.1.call-done = bf16[16,512,64]{1,2,0:T(8,128)(2,1)} async-done(((bf16[2,512,64]{1,2,0:T(8,128)(2,1)}), bf16[16,512,64]{1,2,0:T(8,128)(2,1)}) %all-gather.5.cloned.1.call-update) | async-done | bytes 1048592 | tf_op jit(solution)/shard_map/all_gather | solution.py:22
  52.1 2.3 copy.61
  54.4 0.0 all-reduce.2.cloned.1.call-start
  54.5 0.1 dynamic_slice.3
  54.6 0.2 select_reduce_fusion
  54.8 0.1 broadcast_subtract_fusion
  54.9 55.8 %all-gather.7.cloned.1.call-done = bf16[64,512,64]{1,2,0:T(8,128)(2,1)} async-done(((bf16[16,512,64]{1,2,0:T(8,128)(2,1)}), bf16[64,512,64]{1,2,0:T(8,128)(2,1)}) %all-gather.7.cloned.1.call-update) | async-done | bytes 4194320 | tf_op jit(solution)/shard_map/all_gather | solution.py:22
  110.7 4.6 copy.60
  115.3 82.6 %all-gather.9.cloned.1.call-done = bf16[4096,1024]{0,1:T(8,128)(2,1)} async-done(((bf16[512,1024]{0,1:T(8,128)(2,1)}), bf16[4096,1024]{0,1:T(8,128)(2,1)}) %all-gather.9.cloned.1.call-update) | async-done | bytes 8388624 | tf_op jit(solution)/shard_map/all_gather | solution.py:67
  197.9 8.2 %fusion.25 = f32[512,16,2,32]{0,3,2,1:T(8,128)S(1)} fusion(bf16[512,4096,1,1]{0,1,3,2:T(8,128)(2,1)} %bitcast.52, bf16[16,2,32,4096]{3,2,1,0:T(8,128)(2,1)} %bitcast.55), kind=kOutput, calls=%fused_computation.35 | convolution fusion | flops 4294967296 | bytes 14680064 | tf_op jit(solution)/shard_map/dot_general | solution.py:68
  206.2 2.7 fusion.2
  208.8 0.1 fusion.8
  208.9 0.2 copy.65
  209.1 0.2 copy.64
  209.3 0.4 fusion.9
  209.7 0.4 fusion.10
  210.1 0.4 fusion.5
  210.5 0.4 fusion.6
  211.0 0.7 maximum_multiply_fusion
  211.7 278.5 %all-reduce.2.cloned.1.call-done = f32[2,8,32,32]{3,1,2,0:T(8,128)} async-done(((f32[2,8,32,32]{3,1,2,0:T(8,128)}), f32[2,8,32,32]{3,1,2,0:T(8,128)}) %all-reduce.2.cloned.1.call-update) | async-done | bytes 65552 | tf_op jit(solution)/shard_map/psum | solution.py:76
  490.3 1.7 copy.68
  (18 shorter events, 0.2 us)
Async XLA Ops:
  6.5 47.9 %copy-start.1 = (f32[1024]{0:T(1024)S(1)}, f32[1024]{0:T(1024)}, u32[]{:S(2)}) copy-start(f32[1024]{0:T(1024)} %param.8) | copy-start | bytes 12292
  6.5 47.9 %copy-start.2 = (s32[1024]{0:T(1024)S(1)}, s32[1024]{0:T(1024)}, u32[]{:S(2)}) copy-start(s32[1024]{0:T(1024)} %param.11) | copy-start | bytes 12292
  6.5 48.0 %copy-start.3 = (s32[32]{0:T(128)S(1)}, s32[32]{0:T(128)}, u32[]{:S(2)}) copy-start(s32[32]{0:T(128)} %param.10) | copy-start | bytes 388
  6.5 48.2 %copy-start.4 = (f32[8]{0:T(128)S(1)}, f32[8]{0:T(128)}, u32[]{:S(2)}) copy-start(f32[8]{0:T(128)} %param.9) | copy-start | bytes 100
  6.5 45.5 %all-gather.5.cloned.1.call-start = ((), (), s32[]{:S(2)}) async-start(), calls=%async_computation | async-start | bytes 1179648 | tf_op jit(solution)/shard_map/all_gather | solution.py:22
  12.0 98.7 %all-gather.7.cloned.1.call-start = ((), (), s32[]{:S(2)}) async-start(), calls=%async_computation.1 | async-start | bytes 5242880 | tf_op jit(solution)/shard_map/all_gather | solution.py:22
  52.1 145.9 %all-gather.9.cloned.1.call-start = ((), (), s32[]{:S(2)}) async-start(), calls=%async_computation.2 | async-start | bytes 9437184 | tf_op jit(solution)/shard_map/all_gather | solution.py:67
  54.4 435.8 %all-reduce.2.cloned.1.call-start = ((), (), s32[]{:S(2)}) async-start(), calls=%async_computation.3 | async-start | bytes 524288 | tf_op jit(solution)/shard_map/psum | solution.py:76
  197.9 8.2 %copy-start = (bf16[512,1024]{0,1:T(8,128)(2,1)S(1)}, bf16[512,1024]{0,1:T(8,128)(2,1)}, u32[]{:S(2)}) copy-start(bf16[512,1024]{0,1:T(8,128)(2,1)} %copy.61) | copy-start | bytes 3145732
Sparse Core Ops, SparseCore 0:
  12.1 39.9 all-gather.4
  54.1 56.5 all-gather.6
  112.8 85.0 all-gather.8
  211.8 278.3 all-reduce.1
where the time goes:
time: 499 us; the launch traced here: 498 us
  waiting for transfers between devices  457 us (92%)
  between operations  13.3 us (3%)
  matrix products  12.6 us (3%)
  local copies, waits for them, and re-layouts  9.7 us (2%)
    psum x1, waiting for transfers between devices, shards(): return lax.psum(partial_value, BLK_GA)  279 us
    all_gather x2, waiting for transfers between devices, all_blocks(): pieces = lax.all_gather(pieces, axes[k], axis=0, tiled=True)  95.9 us
    all_gather x1, waiting for transfers between devices, shards(): gathered = lax.all_gather(pair_elements, 'ga', axis=0, tiled=True)  82.6 us
  transfers between devices with their start and end apart: 4, of which 4 were waited for; matrix products, arithmetic and copies ran while one was open for 1% of the time, Pallas kernels for 0%

commit v1 on v0

--- a/solution.py
+++ b/solution.py
@@ -64,7 +64,8 @@
 def shards(pair_elements, screening, energies, frequencies, qp_index, occupied):
     col_count = pair_elements.shape[1]
     band_count = col_count // (2 * STATES)
-    gathered = lax.all_gather(pair_elements, "ga", axis=0, tiled=True)
+    sent = jnp.stack([pair_elements] * lax.axis_size("ga"))
+    gathered = jnp.concatenate(lax.all_to_all(sent, "ga", 0, 0), axis=0)
     screened = jnp.dot(
         gathered_by_axis(screening, BLK, (2, 0, 1), 1), gathered, preferred_element_type=jnp.float32
     )

time: 499 us -> 610 us (1.22)
  blocking collectives: 4.68 us -> 184 us
  waiting for transfers between devices: 457 us -> 368 us
  local copies, waits for them, and re-layouts: 9.7 us -> 20.9 us
  starting transfers between devices: 0.16 us -> 11.2 us
    all_gather x1, blocking collectives: 4.68 us -> 184 us  [all_blocks(): pieces = lax.all_gather(pieces, axes[k], axis=0, tiled=True)]
    all_gather x1 -> x0, waiting for transfers between devices: 82.6 us -> none  [shards(): gathered = lax.all_gather(pair_elements, 'ga', axis=0, tiled=True)]
    all_to_all x0 -> x1, starting transfers between devices: none -> 11.1 us  [shards(): gathered = jnp.concatenate(lax.all_to_all(sent, 'ga', 0, 0), axis=0)]
    reshape x0 -> x1, local copies, waits for them, and re-layouts: none -> 8.06 us  [shards(): gathered = jnp.concatenate(lax.all_to_all(sent, 'ga', 0, 0), axis=0)]
  transfers between devices with their start and end apart: 4 -> 4, of which waited for: 4 -> 3; matrix products, arithmetic and copies ran while one was open for 1% -> 1% of each run, Pallas kernels for 0% -> 0%
where the time goes in v1:
time: 610 us
  waiting for transfers between devices  368 us (60%)
  blocking collectives  184 us (30%)
  local copies, waits for them, and re-layouts  20.9 us (3%)
  between operations  13.2 us (2%)
  starting transfers between devices  11.2 us (2%)
  matrix products  11.2 us (2%)
    psum x1, waiting for transfers between devices, shards(): return lax.psum(partial_value, BLK_GA)  275 us
    all_gather x1, blocking collectives, all_blocks(): pieces = lax.all_gather(pieces, axes[k], axis=0, tiled=True)  184 us
    all_gather x2, waiting for transfers between devices, all_blocks(): pieces = lax.all_gather(pieces, axes[k], axis=0, tiled=True)  93.1 us
  transfers between devices with their start and end apart: 4, of which 3 were waited for; matrix products, arithmetic and copies ran while one was open for 1% of the time, Pallas kernels for 0%

profile of v1, /device:TPU:23, one launch (start us, length us, event | category | flops | bytes accessed | tf_op | source)
XLA Modules:
  0.0 609.5 jit_solution(14493006280054148543)
XLA Ops:
  6.5 1.5 copy.63
  8.0 4.0 stack.8
  12.0 11.1 %all-to-all-start = ((bf16[8,512,1024]{1,2,0:T(8,128)(2,1)}), bf16[8,512,1024]{1,2,0:T(8,128)(2,1)}, u32[]{:S(2)}, u32[]{:S(2)}) async-start(bf16[8,512,1024]{1,2,0:T(8,128)(2,1)} %stack.8), calls=%async_computation | async-start | bytes 16777216 | tf_op jit(solution)/shard_map/all_to_all | solution.py:68
  23.1 183.9 %all-gather = bf16[1024,64]{0,1:T(8,128)(2,1)S(1)} all-gather(bf16[512,64]{0,1:T(8,128)(2,1)S(1)} %copy-done.1), channel_id=2, replica_groups=mesh['blk_0'=8,'blk_1'=4,'blk_2'=2,'ga'=8] {'blk_2'}, dimensions={0}, use_global_device_ids=true | all-gather | bytes 196608 | tf_op jit(solution)/shard_map/all_gather | solution.py:22
  207.1 0.7 copy.79
  207.8 34.9 %all-gather.4.cloned.1.call-done = bf16[16,512,64]{1,2,0:T(8,128)(2,1)} async-done(((bf16[2,512,64]{1,2,0:T(8,128)(2,1)}), bf16[16,512,64]{1,2,0:T(8,128)(2,1)}) %all-gather.4.cloned.1.call-update) | async-done | bytes 1048592 | tf_op jit(solution)/shard_map/all_gather | solution.py:22
  242.8 0.1 dynamic_slice.3
  242.9 0.2 select_reduce_fusion
  243.1 0.1 broadcast_subtract_fusion
  243.2 58.2 %all-gather.6.cloned.1.call-done = bf16[64,512,64]{1,2,0:T(8,128)(2,1)} async-done(((bf16[16,512,64]{1,2,0:T(8,128)(2,1)}), bf16[64,512,64]{1,2,0:T(8,128)(2,1)}) %all-gather.6.cloned.1.call-update) | async-done | bytes 4194320 | tf_op jit(solution)/shard_map/all_gather | solution.py:22
  301.4 4.6 copy.62
  306.0 8.1 %copy.77 = bf16[8,128,8,512]{3,2,0,1:T(8,128)(2,1)} copy(bf16[8,128,8,512]{3,2,1,0:T(8,128)(2,1)} %bitcast.32) | data formatting | bytes 16777216 | tf_op jit(solution)/shard_map/reshape | solution.py:68
  314.1 6.9 %fusion.25 = f32[512,16,2,32]{0,3,2,1:T(8,128)S(1)} fusion(bf16[512,4096,1,1]{0,1,3,2:T(8,128)(2,1)S(1)} %bitcast.56, bf16[16,2,32,4096]{3,2,1,0:T(8,128)(2,1)} %bitcast.54), kind=kOutput, calls=%fused_computation.35 | convolution fusion | flops 4294967296 | bytes 14680064 | tf_op jit(solution)/shard_map/dot_general | solution.py:69
  320.9 2.7 fusion.2
  323.7 0.1 fusion.8
  323.7 0.2 copy.67
  323.9 0.2 copy.68
  324.1 0.4 fusion.10
  324.5 0.4 fusion.9
  324.9 0.4 fusion.6
  325.3 0.4 fusion.5
  325.8 0.7 maximum_multiply_fusion
  326.5 274.8 %all-reduce.2.cloned.1.call-done = f32[2,8,32,32]{3,1,2,0:T(8,128)} async-done(((f32[2,8,32,32]{3,1,2,0:T(8,128)}), f32[2,8,32,32]{3,1,2,0:T(8,128)}) %all-reduce.2.cloned.1.call-update) | async-done | bytes 65552 | tf_op jit(solution)/shard_map/psum | solution.py:77
  601.3 1.7 copy.71
  (21 shorter events, 0.2 us)
Async XLA Ops:
  12.0 11.1 %copy-start.1 = (bf16[512,64]{0,1:T(8,128)(2,1)S(1)}, bf16[512,64]{0,1:T(8,128)(2,1)}, u32[]{:S(2)}) copy-start(bf16[512,64]{0,1:T(8,128)(2,1)} %param.7) | copy-start | bytes 196612
  12.0 230.8 %copy-start.2 = (f32[1024]{0:T(1024)S(1)}, f32[1024]{0:T(1024)}, u32[]{:S(2)}) copy-start(f32[1024]{0:T(1024)} %param.8) | copy-start | bytes 12292
  12.0 230.8 %copy-start.3 = (s32[1024]{0:T(1024)S(1)}, s32[1024]{0:T(1024)}, u32[]{:S(2)}) copy-start(s32[1024]{0:T(1024)} %param.11) | copy-start | bytes 12292
  12.0 230.9 %copy-start.4 = (s32[32]{0:T(128)S(1)}, s32[32]{0:T(128)}, u32[]{:S(2)}) copy-start(s32[32]{0:T(128)} %param.10) | copy-start | bytes 388
  12.0 231.1 %copy-start.5 = (f32[8]{0:T(128)S(1)}, f32[8]{0:T(128)}, u32[]{:S(2)}) copy-start(f32[8]{0:T(128)} %param.9) | copy-start | bytes 100
  12.0 294.0 %all-to-all-start = ((bf16[8,512,1024]{1,2,0:T(8,128)(2,1)}), bf16[8,512,1024]{1,2,0:T(8,128)(2,1)}, u32[]{:S(2)}, u32[]{:S(2)}) async-start(bf16[8,512,1024]{1,2,0:T(8,128)(2,1)} %stack.8), calls=%async_computation | async-start | bytes 16777216 | tf_op jit(solution)/shard_map/all_to_all | solution.py:68
  23.1 219.6 %all-gather.4.cloned.1.call-start = ((), (), s32[]{:S(2)}) async-start(), calls=%async_computation.1 | async-start | bytes 1179648 | tf_op jit(solution)/shard_map/all_gather | solution.py:22
  207.8 93.6 %all-gather.6.cloned.1.call-start = ((), (), s32[]{:S(2)}) async-start(), calls=%async_computation.2 | async-start | bytes 5242880 | tf_op jit(solution)/shard_map/all_gather | solution.py:22
  242.7 358.6 %all-reduce.2.cloned.1.call-start = ((), (), s32[]{:S(2)}) async-start(), calls=%async_computation.3 | async-start | bytes 524288 | tf_op jit(solution)/shard_map/psum | solution.py:77
  306.0 8.1 %copy-start = (bf16[8,4,2,512,64]{3,4,2,1,0:T(8,128)(2,1)S(1)}, bf16[8,4,2,512,64]{3,4,2,1,0:T(8,128)(2,1)}, u32[]{:S(2)}) copy-start(bf16[8,4,2,512,64]{3,4,2,1,0:T(8,128)(2,1)} %copy.62) | copy-start | bytes 12582916
Sparse Core Ops, SparseCore 0:
  207.9 34.7 all-gather.3
  244.8 56.5 all-gather.5
  326.6 274.6 all-reduce.1
